TPU v7x, 256 devices: a whole 4x4x8 slice. The times are simulated.
256 devices in a mesh: grp: 4 (over y), col: 64 (over x, z, core).
Axes of the slice: x: 4, y: 4, z: 8, core: 2. Of those that a mesh axis runs over, the one named last changes fastest.
Arguments:
- panels: bfloat16 [256, 4, 512, 512], P('col', None, 'grp'), may hold values from -1.296875 to 1.296875
- parent: float32 [256, 512, 512], P('col', 'grp'), may hold values from -6 to 6
- src_block: int32 [64, 40], P('col'), may hold values from 0 to 39, each once within a row
- dest_owner: int32 [2560, 1], P('col'), may hold values from 0 to 63; in each aligned block of 40 rows (0 to 39, 40 to 79, ...) no two rows name the same one
- target: int32 [2560], P('col'), may hold values from 0 to 3
- counts: int32 [64], P('col'), may hold values from 20 to 40, as said below
Outputs:
- assembled: float32 [256, 512, 512], P('col', 'grp')
Inputs may be any that keep to these rules, and one draw needn't show every extreme that they name: `src_block`: each row of a column rank is a permutation of the 40 block pairs. `dest_owner`: among the 40 slots of one column rank at most 1 name the same owner. The live slots of a rank are its first counts[c]; some rank has all 40 live.
All inputs are finite; a program needn't handle non-finite values.
Results may differ from a plain program's by a relative error of at most 0.0026.
Values may be sent and summed in bfloat16 or wider, within the bound.
A program may use at most 128 MiB of HBM per device.

v0:
```python
import jax
import jax.numpy as jnp
import numpy as np
from jax import lax
from jax.sharding import PartitionSpec as P


def place_slots(src_block, dest_owner, target, counts, peer_count, capacity):
    slot_count = src_block.shape[1]
    slot_index = jnp.arange(slot_count, dtype=jnp.int32)
    owner_rank = dest_owner[:, 0]
    matches = (owner_rank[:, None] == jnp.arange(peer_count, dtype=jnp.int32)[None, :]).astype(
        jnp.int32
    )
    earlier = jnp.cumsum(matches, axis=0) - matches
    rank_in = jnp.sum(earlier * matches, axis=1)
    position = owner_rank * capacity + rank_in
    is_live = slot_index < counts[0]
    routed = jnp.zeros((peer_count * capacity,), jnp.int32).at[position].set(target)
    return (src_block[0], position, is_live, routed.reshape(peer_count, capacity))


def pack_updates(flat_updates, chosen, position, is_live, peer_count, capacity):
    picked = flat_updates[chosen]
    picked = jnp.where(is_live[:, None, None], picked, jnp.zeros_like(picked))
    buffer = (
        jnp.zeros((peer_count * capacity,) + picked.shape[1:], picked.dtype)
        .at[position]
        .set(picked)
    )
    return buffer.reshape((peer_count, capacity) + picked.shape[1:])


def assemble(received, labels, targets):
    arrived = received.reshape((-1,) + received.shape[2:])
    flat_labels = labels.reshape(-1)
    select = (flat_labels[None, :] == jnp.arange(targets, dtype=jnp.int32)[:, None]).astype(
        jnp.bfloat16
    )
    return jnp.einsum("tn,nrc->trc", select, arrived, preferred_element_type=jnp.float32)


def pair_products(own_rows, piece_rows):
    blocks = own_rows.shape[1]
    upper_table = np.array([a for a in range(blocks) for b in range(a + 1)], np.int32)
    lower_table = np.array([b for a in range(blocks) for b in range(a + 1)], np.int32)
    left_rows = own_rows[:, upper_table]
    right_rows = piece_rows[:, lower_table]
    return jnp.einsum(
        "fprw,fpcw->fprc", left_rows, right_rows, preferred_element_type=jnp.float32
    ).astype(jnp.bfloat16)


def per_device(panels, parent, src_block, dest_owner, target, counts):
    fronts, blocks, quarter, _ = panels.shape
    pair_count = blocks * (blocks + 1) // 2
    peer_count = lax.axis_size("col")
    slot_count = src_block.shape[1]
    capacity = (slot_count + peer_count - 1) // peer_count + slot_count // (2 * peer_count)
    targets = parent.shape[0]
    chosen, position, is_live, routed = place_slots(
        src_block, dest_owner, target, counts, peer_count, capacity
    )
    products = pair_products(panels, lax.all_gather(panels, "grp", axis=2, tiled=True))
    flat_updates = products.reshape(fronts * pair_count, quarter, products.shape[3])
    buffer = pack_updates(flat_updates, chosen, position, is_live, peer_count, capacity)
    received, labels = (
        lax.all_to_all(buffer, "col", split_axis=0, concat_axis=0, tiled=True),
        lax.all_to_all(routed, "col", split_axis=0, concat_axis=0, tiled=True),
    )
    return parent - assemble(received, labels, targets)


def solution(mesh):
    placed = (
        P("col", None, "grp", None),
        P("col", "grp", None),
        P("col", None),
        P("col", None),
        P("col"),
        P("col"),
    )
    return jax.shard_map(
        per_device, mesh=mesh, in_specs=placed, out_specs=P("col", "grp", None), check_vma=False
    )
```

profile of v0, /device:TPU:1, one launch (start us, length us, event | category | flops | bytes accessed | tf_op | source)
XLA Modules:
  0.0 390.6 jit_solution(11302547754613624316)
XLA Ops:
  6.5 0.7 all-gather.2.cloned.1.call-update
  7.3 0.7 fusion.13
  8.1 0.8 select_reduce_fusion
  8.9 0.7 fusion.17
  9.6 0.8 scatter_custom_fusion
  10.4 0.7 copy.36
  11.1 13.0 %all-to-all-start = ((s32[64,1,1]{2,1,0:T(1,128)}), s32[64,1,1]{2,1,0:T(1,128)S(1)}, u32[]{:S(2)}, u32[]{:S(2)}) async-start(s32[64,1,1]{2,1,0:T(1,128)} %copy.36), calls=%async_computation | async-start | bytes 65536 | tf_op jit(solution)/shard_map/all_to_all | solution.py:69
  24.1 0.7 pad_clamp_fusion.2
  24.8 5.7 %gather_fusion = bf16[10,4,128,512]{3,2,1,0:T(8,128)(2,1)} fusion(bf16[4,4,128,512]{3,2,1,0:T(8,128)(2,1)} %param.10, s32[1024]{0:T(1024)S(1)} %pad_clamp_fusion.2), kind=kCustom, calls=%fused_computation | custom fusion | bytes 10485800 | tf_op jit(solution)/shard_map/gather | solution.py:47
  31.2 67.3 %all-gather.2.cloned.1.call-done = bf16[4,4,512,512]{3,2,1,0:T(8,128)(2,1)} async-done(((bf16[4,4,128,512]{3,2,1,0:T(8,128)(2,1)}), bf16[4,4,512,512]{3,2,1,0:T(8,128)(2,1)}) %all-gather.2.cloned.1.call-update) | async-done | bytes 8388624 | tf_op jit(solution)/shard_map/all_gather | solution.py:64
  98.4 6.0 %fusion.22 = (bf16[4,4,256,512]{3,2,1,0:T(8,128)(2,1)}, bf16[4,4,256,512]{3,2,1,0:T(8,128)(2,1)}) fusion(bf16[4,4,512,512]{3,2,1,0:T(8,128)(2,1)} %all-gather.2.cloned.1.call-done), kind=kLoop, calls=%fused_computation.37 | loop fusion | bytes 16777216 | tf_op jit(solution)/shard_map/gather | solution.py:48
  104.5 7.6 %gather_fusion.2 = bf16[10,4,256,512]{3,2,1,0:T(8,128)(2,1)} fusion(bf16[4,4,256,512]{3,2,1,0:T(8,128)(2,1)} %get-tuple-element.5, s32[1024]{0:T(1024)S(1)} %pad_clamp_fusion.1), kind=kCustom, calls=%fused_computation.2 | custom fusion | bytes 20971560 | tf_op jit(solution)/shard_map/gather | solution.py:48
  112.1 7.7 %gather_fusion.3 = bf16[10,4,256,512]{3,2,1,0:T(8,128)(2,1)} fusion(bf16[4,4,256,512]{3,2,1,0:T(8,128)(2,1)} %get-tuple-element.6, s32[1024]{0:T(1024)S(1)} %pad_clamp_fusion.1), kind=kCustom, calls=%fused_computation.3 | custom fusion | bytes 20971560 | tf_op jit(solution)/shard_map/gather | solution.py:48
  119.7 12.3 %copy_bitcast_fusion = (bf16[4,10,256,512]{3,2,1,0:T(8,128)(2,1)S(1)}, bf16[4,10,256,512]{3,2,1,0:T(8,128)(2,1)}) fusion(bf16[10,4,256,512]{3,2,1,0:T(8,128)(2,1)} %gather_fusion.3, bf16[10,4,256,512]{3,2,1,0:T(8,128)(2,1)} %gather_fusion.2), kind=kLoop, calls=%fused_computation.10 | loop fusion | bytes 41943040 | tf_op jit(solution)/shard_map/gather | solution.py:48
  132.1 10.5 %fusion.8 = bf16[4,10,128,512]{3,2,1,0:T(8,128)(2,1)} fusion(bf16[4,10,256,512]{3,2,1,0:T(8,128)(2,1)S(1)} %get-tuple-element.7, bf16[4,10,256,512]{3,2,1,0:T(8,128)(2,1)} %get-tuple-element.8, bf16[10,4,128,512]{3,2,1,0:T(8,128)(2,1)S(1)} %bitcast.34), kind=kOutput, calls=%fused_computation.17 | convolution fusion | flops 2728919040 | bytes 31457280 | tf_op jit(solution)/shard_map/fprw,fpcw->fprc/dot_general | solution.py:49
  142.6 7.2 %gather_fusion.1 = bf16[40,128,512]{2,1,0:T(8,128)(2,1)} fusion(bf16[40,128,512]{2,1,0:T(8,128)(2,1)} %bitcast.35, s32[1024]{0:T(1024)S(1)} %pad_clamp_fusion), kind=kCustom, calls=%fused_computation.1 | custom fusion | bytes 10485920 | tf_op jit(solution)/shard_map/gather | solution.py:24
  149.8 5.3 %broadcast_select_fusion = bf16[40,128,512]{2,1,0:T(8,128)(2,1)} fusion(bf16[40,128,512]{2,1,0:T(8,128)(2,1)} %gather_fusion.1, pred[40]{0:T(512)(128)(4,1)S(1)} %iota_compare_fusion.2), kind=kLoop, calls=%fused_computation.16 | loop fusion | flops 2621440 | bytes 10485800 | tf_op jit(solution)/shard_map/jit(_where)/select_n | solution.py:25
  155.1 4.2 %broadcast_in_dim.30 = bf16[64,128,512]{2,1,0:T(8,128)(2,1)} broadcast(bf16[]{:T(256)} %constant.10.clone.1), dimensions={} | broadcast | bytes 8388610 | tf_op jit(solution)/shard_map/broadcast_in_dim | solution.py:27
  159.3 14.1 %scatter_fusion = bf16[64,128,512]{2,1,0:T(8,128)(2,1)} fusion(bf16[64,128,512]{2,1,0:T(8,128)(2,1)} %broadcast_in_dim.30, s32[40]{0:T(128)S(1)} %fusion.17, bf16[40,128,512]{2,1,0:T(8,128)(2,1)} %broadcast_select_fusion), kind=kCustom, calls=%fused_computation.5 | custom fusion | bytes 15728800 | tf_op jit(solution)/shard_map/scatter | solution.py:29
  173.4 11.0 %all-to-all-start.1 = ((bf16[64,1,128,512]{3,2,1,0:T(8,128)(2,1)}), bf16[64,1,128,512]{3,2,1,0:T(8,128)(2,1)}, u32[]{:S(2)}, u32[]{:S(2)}) async-start(bf16[64,1,128,512]{3,2,1,0:T(8,128)(2,1)} %bitcast.32), calls=%async_computation.1 | async-start | bytes 16777216 | tf_op jit(solution)/shard_map/all_to_all | solution.py:68
  184.4 1.2 reduce
  185.6 184.5 %all-to-all-done.1 = bf16[64,1,128,512]{3,2,1,0:T(8,128)(2,1)} async-done(((bf16[64,1,128,512]{3,2,1,0:T(8,128)(2,1)}), bf16[64,1,128,512]{3,2,1,0:T(8,128)(2,1)}, u32[]{:S(2)}, u32[]{:S(2)}) %all-to-all-start.1) | async-done | bytes 8388640 | tf_op jit(solution)/shard_map/all_to_all | solution.py:68
  370.1 12.3 %fusion.4 = f32[4,128,512]{2,0,1:T(4,128)S(1)} fusion(bf16[64,1,128,512]{3,2,1,0:T(8,128)(2,1)} %all-to-all-done.1, s32[64]{0:T(128)S(1)} %reduce), kind=kOutput, calls=%fused_computation.12 | convolution fusion | flops 33554688 | bytes 9437440 | tf_op jit(solution)/shard_map/tn,nrc->trc/dot_general | solution.py:40
  382.3 1.4 copy_subtract_fusion
  (18 shorter events, 0.1 us)
Async XLA Ops:
  6.5 24.6 %copy-start.1 = (s32[10]{0:T(128)S(1)}, s32[10]{0:T(128)}, u32[]{:S(2)}) copy-start(s32[10]{0:T(128)} %constant.35) | copy-start | bytes 124
  6.5 24.6 %copy-start.2 = (s32[1,40]{1,0:T(1,128)S(1)}, s32[1,40]{1,0:T(1,128)}, u32[]{:S(2)}) copy-start(s32[1,40]{1,0:T(1,128)} %param.12) | copy-start | bytes 484
  6.5 91.9 %all-gather.2.cloned.1.call-start = ((), (), s32[]{:S(2)}) async-start(), calls=%async_computation.2 | async-start | bytes 10485760 | tf_op jit(solution)/shard_map/all_gather | solution.py:64
  11.1 162.3 %all-to-all-start = ((s32[64,1,1]{2,1,0:T(1,128)}), s32[64,1,1]{2,1,0:T(1,128)S(1)}, u32[]{:S(2)}, u32[]{:S(2)}) async-start(s32[64,1,1]{2,1,0:T(1,128)} %copy.36), calls=%async_computation | async-start | bytes 65536 | tf_op jit(solution)/shard_map/all_to_all | solution.py:69
  112.1 20.0 %slice-start = ((s8[5242880]{0:T(1024)(128)(4,1)}), s8[1048576]{0:T(1024)(128)(4,1)S(1)}, s32[]{:S(2)}) async-start(s8[5242880]{0:T(1024)(128)(4,1)} %bitcast.33), calls=%async_computation.3 | async-start | bytes 2097152
  119.7 12.4 %slice-start.1 = ((s8[5242880]{0:T(1024)(128)(4,1)}), s8[4194304]{0:T(1024)(128)(4,1)S(1)}, s32[]{:S(2)}) async-start(s8[5242880]{0:T(1024)(128)(4,1)} %bitcast.33), calls=%async_computation.4 | async-start | bytes 8388608
  173.4 196.7 %all-to-all-start.1 = ((bf16[64,1,128,512]{3,2,1,0:T(8,128)(2,1)}), bf16[64,1,128,512]{3,2,1,0:T(8,128)(2,1)}, u32[]{:S(2)}, u32[]{:S(2)}) async-start(bf16[64,1,128,512]{3,2,1,0:T(8,128)(2,1)} %bitcast.32), calls=%async_computation.1 | async-start | bytes 16777216 | tf_op jit(solution)/shard_map/all_to_all | solution.py:68
  184.3 198.0 %copy-start = (f32[4,128,512]{2,1,0:T(8,128)S(1)}, f32[4,128,512]{2,1,0:T(8,128)}, u32[]{:S(2)}) copy-start(f32[4,128,512]{2,1,0:T(8,128)} %param.11) | copy-start | bytes 3145732
Sparse Core Ops, SparseCore 0:
  9.1 89.2 all-gather.1
where the time goes:
time: 391 us
  waiting for transfers between devices  252 us (64%)
  local copies, waits for them, and re-layouts  66.4 us (17%)
  starting transfers between devices  23.9 us (6%)
  matrix products  22.8 us (6%)
  between operations  14.1 us (4%)
  other arithmetic  10.9 us (3%)
    all_to_all x1, waiting for transfers between devices, per_device(): lax.all_to_all(buffer, 'col', split_axis=0, concat_axis=0, tiled=True)  184 us
    all_gather x1, waiting for transfers between devices, per_device(): lax.all_gather(panels, 'grp', axis=2, tiled=True)  67.3 us
    gather x4, local copies, waits for them, and re-layouts, pair_products(): right_rows = piece_rows[:, lower_table]  33.6 us
    scatter x1, local copies, waits for them, and re-layouts, pack_updates(): buffer = jnp.zeros((peer_count * capacity,) + picked.shape[1:], picked.dt...  14.1 us
    all_to_all x1, starting transfers between devices, per_device(): lax.all_to_all(routed, 'col', split_axis=0, concat_axis=0, tiled=True)  13 us
    dot_general x1, matrix products, assemble(): jnp.einsum('tn,nrc->trc', select, arrived, preferred_element_type=jnp.flo...  12.3 us
    all_to_all x1, starting transfers between devices, per_device(): lax.all_to_all(buffer, 'col', split_axis=0, concat_axis=0, tiled=True)  11 us
    dot_general x1, matrix products, pair_products(): jnp.einsum('fprw,fpcw->fprc', left_rows, right_rows, preferred_element_ty...  10.5 us
  transfers between devices with their start and end apart: 3, of which 2 were waited for; matrix products, arithmetic and copies ran while one was open for 22% of the time, Pallas kernels for 0%

commit v1 on v0

--- a/solution.py
+++ b/solution.py
@@ -1,8 +1,25 @@
+import functools
 import jax
 import jax.numpy as jnp
 import numpy as np
 from jax import lax
 from jax.sharding import PartitionSpec as P
+from jax.lax import all_to_all, axis_size
+
+
+def _open_paths(shard_in, mesh_name, array_axis):
+    return jnp.concatenate(
+        all_to_all(
+            jnp.stack([shard_in] * axis_size(mesh_name), axis=0),
+            concat_axis=0,
+            axis_name=mesh_name,
+            split_axis=0,
+        ),
+        axis=array_axis,
+    )
+
+
+order_rounds = functools.partial(_open_paths, mesh_name="grp", array_axis=2)
 
 
 def place_slots(src_block, dest_owner, target, counts, peer_count, capacity):
@@ -61,7 +78,7 @@
     chosen, position, is_live, routed = place_slots(
         src_block, dest_owner, target, counts, peer_count, capacity
     )
-    products = pair_products(panels, lax.all_gather(panels, "grp", axis=2, tiled=True))
+    products = pair_products(panels, order_rounds(panels))
     flat_updates = products.reshape(fronts * pair_count, quarter, products.shape[3])
     buffer = pack_updates(flat_updates, chosen, position, is_live, peer_count, capacity)
     received, labels = (

time: 391 us -> 412 us (1.054)
  waiting for transfers between devices: 252 us -> 270 us
  between operations: 14.1 us -> 0.8 us
  local copies, waits for them, and re-layouts: 66.4 us -> 77.9 us
  starting transfers between devices: 23.9 us -> 31 us
    all_to_all x0 -> x1, waiting for transfers between devices: none -> 85.8 us  [_open_paths(): all_to_all(jnp.stack([shard_in] * axis_size(mesh_name), axis=0), concat_a...]
    all_gather x1 -> x0, waiting for transfers between devices: 67.3 us -> none  [per_device(): lax.all_gather(panels, 'grp', axis=2, tiled=True)]
    all_to_all x0 -> x1, local copies, waits for them, and re-layouts: none -> 7.59 us  [_open_paths(): all_to_all(jnp.stack([shard_in] * axis_size(mesh_name), axis=0), concat_a...]
    another operation x0 -> x1, local copies, waits for them, and re-layouts: none -> 5.98 us  [_open_paths(): jnp.stack([shard_in] * axis_size(mesh_name), axis=0)]
    all_to_all x0 -> x1, starting transfers between devices: none -> 5.77 us  [_open_paths(): all_to_all(jnp.stack([shard_in] * axis_size(mesh_name), axis=0), concat_a...]
where the time goes in v1:
time: 412 us; the launch traced here: 411 us
  waiting for transfers between devices  270 us (66%)
  local copies, waits for them, and re-layouts  77.9 us (19%)
  starting transfers between devices  31 us (8%)
  matrix products  22.8 us (6%)
  other arithmetic  8.25 us (2%)
    all_to_all x1, waiting for transfers between devices, per_device(): lax.all_to_all(buffer, 'col', split_axis=0, concat_axis=0, tiled=True)  184 us
    all_to_all x1, waiting for transfers between devices, _open_paths(): all_to_all(jnp.stack([shard_in] * axis_size(mesh_name), axis=0), concat_a...  85.8 us
    gather x4, local copies, waits for them, and re-layouts, pair_products(): right_rows = piece_rows[:, lower_table]  33.5 us
    all_to_all x1, starting transfers between devices, per_device(): lax.all_to_all(routed, 'col', split_axis=0, concat_axis=0, tiled=True)  14.9 us
    scatter x1, local copies, waits for them, and re-layouts, pack_updates(): buffer = jnp.zeros((peer_count * capacity,) + picked.shape[1:], picked.dt...  14.1 us
    dot_general x1, matrix products, assemble(): jnp.einsum('tn,nrc->trc', select, arrived, preferred_element_type=jnp.flo...  12.3 us
    dot_general x1, matrix products, pair_products(): jnp.einsum('fprw,fpcw->fprc', left_rows, right_rows, preferred_element_ty...  10.5 us
    all_to_all x1, starting transfers between devices, per_device(): lax.all_to_all(buffer, 'col', split_axis=0, concat_axis=0, tiled=True)  10.4 us
  transfers between devices with their start and end apart: 3, of which 2 were waited for; matrix products, arithmetic and copies ran while one was open for 22% of the time, Pallas kernels for 0%

profile of v1, /device:TPU:1, one launch (start us, length us, event | category | flops | bytes accessed | tf_op | source)
XLA Modules:
  0.0 411.0 jit_solution(55861167895573299)
XLA Ops:
  0.0 6.0 %stack.2 = bf16[4,4,4,128,512]{4,3,2,1,0:T(8,128)(2,1)} broadcast(bf16[4,4,128,512]{3,2,1,0:T(8,128)(2,1)} %param.10), dimensions={1,2,3,4} | broadcast | bytes 10485760 | tf_op jit(solution)/shard_map/stack | solution.py:13
  6.0 5.8 %all-to-all-start.1 = ((bf16[4,4,4,128,512]{4,3,2,1,0:T(8,128)(2,1)}), bf16[4,4,4,128,512]{4,3,2,1,0:T(8,128)(2,1)}, u32[]{:S(2)}, u32[]{:S(2)}) async-start(bf16[4,4,4,128,512]{4,3,2,1,0:T(8,128)(2,1)} %stack.2), calls=%async_computation.1 | async-start | bytes 16777216 | tf_op jit(solution)/shard_map/all_to_all | solution.py:12
  11.8 3.8 gather_fusion
  16.3 0.1 fusion.13
  16.4 0.2 select_reduce_fusion
  16.6 0.8 scatter_custom_fusion
  17.4 0.7 copy.38
  18.2 85.8 %all-to-all-done.1 = bf16[4,4,4,128,512]{4,3,2,1,0:T(8,128)(2,1)} async-done(((bf16[4,4,4,128,512]{4,3,2,1,0:T(8,128)(2,1)}), bf16[4,4,4,128,512]{4,3,2,1,0:T(8,128)(2,1)}, u32[]{:S(2)}, u32[]{:S(2)}) %all-to-all-start.1) | async-done | bytes 8388640 | tf_op jit(solution)/shard_map/all_to_all | solution.py:12
  104.0 14.9 %all-to-all-start = ((s32[64,1,1]{2,1,0:T(1,128)}), s32[64,1,1]{2,1,0:T(1,128)S(1)}, u32[]{:S(2)}, u32[]{:S(2)}) async-start(s32[64,1,1]{2,1,0:T(1,128)} %copy.38), calls=%async_computation | async-start | bytes 65536 | tf_op jit(solution)/shard_map/all_to_all | solution.py:86
  118.8 7.6 %copy.39 = bf16[4,4,4,128,512]{4,3,0,2,1:T(8,128)(2,1)} copy(bf16[4,4,4,128,512]{4,3,2,1,0:T(8,128)(2,1)} %all-to-all-done.1) | data formatting | bytes 16777216 | tf_op jit(solution)/shard_map/all_to_all | solution.py:12
  126.4 5.8 %fusion.22 = (bf16[4,4,256,512]{3,2,1,0:T(8,128)(2,1)}, bf16[4,4,256,512]{3,2,1,0:T(8,128)(2,1)}) fusion(bf16[4,4,512,512]{3,2,1,0:T(8,128)(2,1)} %bitcast.36), kind=kLoop, calls=%fused_computation.37 | loop fusion | bytes 16777216 | tf_op jit(solution)/shard_map/gather | solution.py:65
  132.2 7.6 %gather_fusion.2 = bf16[10,4,256,512]{3,2,1,0:T(8,128)(2,1)} fusion(bf16[4,4,256,512]{3,2,1,0:T(8,128)(2,1)} %get-tuple-element.5, s32[1024]{0:T(1024)S(1)} %pad_clamp_fusion.1), kind=kCustom, calls=%fused_computation.2 | custom fusion | bytes 20971560 | tf_op jit(solution)/shard_map/gather | solution.py:65
  139.8 7.7 %gather_fusion.3 = bf16[10,4,256,512]{3,2,1,0:T(8,128)(2,1)} fusion(bf16[4,4,256,512]{3,2,1,0:T(8,128)(2,1)} %get-tuple-element.6, s32[1024]{0:T(1024)S(1)} %pad_clamp_fusion.1), kind=kCustom, calls=%fused_computation.3 | custom fusion | bytes 20971560 | tf_op jit(solution)/shard_map/gather | solution.py:65
  147.5 12.4 %copy_bitcast_fusion = (bf16[4,10,256,512]{3,2,1,0:T(8,128)(2,1)S(1)}, bf16[4,10,256,512]{3,2,1,0:T(8,128)(2,1)}) fusion(bf16[10,4,256,512]{3,2,1,0:T(8,128)(2,1)} %gather_fusion.3, bf16[10,4,256,512]{3,2,1,0:T(8,128)(2,1)} %gather_fusion.2), kind=kLoop, calls=%fused_computation.10 | loop fusion | bytes 41943040 | tf_op jit(solution)/shard_map/gather | solution.py:65
  159.9 10.5 %fusion.8 = bf16[4,10,128,512]{3,2,1,0:T(8,128)(2,1)} fusion(bf16[4,10,256,512]{3,2,1,0:T(8,128)(2,1)S(1)} %get-tuple-element.7, bf16[4,10,256,512]{3,2,1,0:T(8,128)(2,1)} %get-tuple-element.8, bf16[10,4,128,512]{3,2,1,0:T(8,128)(2,1)S(1)} %bitcast.38), kind=kOutput, calls=%fused_computation.17 | convolution fusion | flops 2728919040 | bytes 31457280 | tf_op jit(solution)/shard_map/fprw,fpcw->fprc/dot_general | solution.py:66
  170.4 7.2 %gather_fusion.1 = bf16[40,128,512]{2,1,0:T(8,128)(2,1)} fusion(bf16[40,128,512]{2,1,0:T(8,128)(2,1)} %bitcast.39, s32[1024]{0:T(1024)S(1)} %pad_clamp_fusion), kind=kCustom, calls=%fused_computation.1 | custom fusion | bytes 10485920 | tf_op jit(solution)/shard_map/gather | solution.py:41
  177.6 5.3 %broadcast_select_fusion = bf16[40,128,512]{2,1,0:T(8,128)(2,1)} fusion(bf16[40,128,512]{2,1,0:T(8,128)(2,1)} %gather_fusion.1, pred[40]{0:T(512)(128)(4,1)S(1)} %iota_compare_fusion.2), kind=kLoop, calls=%fused_computation.16 | loop fusion | flops 2621440 | bytes 10485800 | tf_op jit(solution)/shard_map/jit(_where)/select_n | solution.py:42
  182.8 4.2 %broadcast_in_dim.30 = bf16[64,128,512]{2,1,0:T(8,128)(2,1)} broadcast(bf16[]{:T(256)} %constant.10.clone.1), dimensions={} | broadcast | bytes 8388610 | tf_op jit(solution)/shard_map/broadcast_in_dim | solution.py:44
  187.1 14.1 %scatter_fusion = bf16[64,128,512]{2,1,0:T(8,128)(2,1)} fusion(bf16[64,128,512]{2,1,0:T(8,128)(2,1)} %broadcast_in_dim.30, s32[40]{0:T(128)S(1)} %fusion.17, bf16[40,128,512]{2,1,0:T(8,128)(2,1)} %broadcast_select_fusion), kind=kCustom, calls=%fused_computation.5 | custom fusion | bytes 15728800 | tf_op jit(solution)/shard_map/scatter | solution.py:46
  201.2 10.4 %all-to-all-start.2 = ((bf16[64,1,128,512]{3,2,1,0:T(8,128)(2,1)}), bf16[64,1,128,512]{3,2,1,0:T(8,128)(2,1)}, u32[]{:S(2)}, u32[]{:S(2)}) async-start(bf16[64,1,128,512]{3,2,1,0:T(8,128)(2,1)} %bitcast.35), calls=%async_computation.2 | async-start | bytes 16777216 | tf_op jit(solution)/shard_map/all_to_all | solution.py:85
  211.6 1.2 reduce
  212.8 184.5 %all-to-all-done.2 = bf16[64,1,128,512]{3,2,1,0:T(8,128)(2,1)} async-done(((bf16[64,1,128,512]{3,2,1,0:T(8,128)(2,1)}), bf16[64,1,128,512]{3,2,1,0:T(8,128)(2,1)}, u32[]{:S(2)}, u32[]{:S(2)}) %all-to-all-start.2) | async-done | bytes 8388640 | tf_op jit(solution)/shard_map/all_to_all | solution.py:85
  397.3 12.3 %fusion.4 = f32[4,128,512]{2,0,1:T(4,128)S(1)} fusion(bf16[64,1,128,512]{3,2,1,0:T(8,128)(2,1)} %all-to-all-done.2, s32[64]{0:T(128)S(1)} %reduce), kind=kOutput, calls=%fused_computation.12 | convolution fusion | flops 33554688 | bytes 9437440 | tf_op jit(solution)/shard_map/tn,nrc->trc/dot_general | solution.py:57
  409.6 1.4 copy_subtract_fusion
  (25 shorter events, 0.1 us)
Async XLA Ops:
  6.0 5.8 %copy-start.4 = (s32[10]{0:T(128)S(1)}, s32[10]{0:T(128)}, u32[]{:S(2)}) copy-start(s32[10]{0:T(128)} %constant.34) | copy-start | bytes 124
  6.0 5.8 %copy-start = (bf16[4,4,128,512]{3,2,1,0:T(8,128)(2,1)S(1)}, bf16[4,4,128,512]{3,2,1,0:T(8,128)(2,1)}, u32[]{:S(2)}) copy-start(bf16[4,4,128,512]{3,2,1,0:T(8,128)(2,1)} %param.10) | copy-start | bytes 6291460
  6.0 98.0 %all-to-all-start.1 = ((bf16[4,4,4,128,512]{4,3,2,1,0:T(8,128)(2,1)}), bf16[4,4,4,128,512]{4,3,2,1,0:T(8,128)(2,1)}, u32[]{:S(2)}, u32[]{:S(2)}) async-start(bf16[4,4,4,128,512]{4,3,2,1,0:T(8,128)(2,1)} %stack.2), calls=%async_computation.1 | async-start | bytes 16777216 | tf_op jit(solution)/shard_map/all_to_all | solution.py:12
  11.8 4.5 %copy-start.2 = (s32[40,1]{0,1:T(1,128)S(1)}, s32[40,1]{0,1:T(1,128)}, u32[]{:S(2)}) copy-start(s32[40,1]{0,1:T(1,128)} %param.13) | copy-start | bytes 484
  11.8 6.4 %copy-start.3 = (s32[10]{0:T(128)S(1)}, s32[10]{0:T(128)}, u32[]{:S(2)}) copy-start(s32[10]{0:T(128)} %constant.35) | copy-start | bytes 124
  11.8 6.4 %copy-start.5 = (s32[1,40]{1,0:T(1,128)S(1)}, s32[1,40]{1,0:T(1,128)}, u32[]{:S(2)}) copy-start(s32[1,40]{1,0:T(1,128)} %param.12) | copy-start | bytes 484
  104.0 97.2 %all-to-all-start = ((s32[64,1,1]{2,1,0:T(1,128)}), s32[64,1,1]{2,1,0:T(1,128)S(1)}, u32[]{:S(2)}, u32[]{:S(2)}) async-start(s32[64,1,1]{2,1,0:T(1,128)} %copy.38), calls=%async_computation | async-start | bytes 65536 | tf_op jit(solution)/shard_map/all_to_all | solution.py:86
  139.8 20.0 %slice-start = ((s8[5242880]{0:T(1024)(128)(4,1)}), s8[1048576]{0:T(1024)(128)(4,1)S(1)}, s32[]{:S(2)}) async-start(s8[5242880]{0:T(1024)(128)(4,1)} %bitcast.37), calls=%async_computation.3 | async-start | bytes 2097152
  147.5 12.4 %slice-start.1 = ((s8[5242880]{0:T(1024)(128)(4,1)}), s8[4194304]{0:T(1024)(128)(4,1)S(1)}, s32[]{:S(2)}) async-start(s8[5242880]{0:T(1024)(128)(4,1)} %bitcast.37), calls=%async_computation.4 | async-start | bytes 8388608
  201.2 196.1 %all-to-all-start.2 = ((bf16[64,1,128,512]{3,2,1,0:T(8,128)(2,1)}), bf16[64,1,128,512]{3,2,1,0:T(8,128)(2,1)}, u32[]{:S(2)}, u32[]{:S(2)}) async-start(bf16[64,1,128,512]{3,2,1,0:T(8,128)(2,1)} %bitcast.35), calls=%async_computation.2 | async-start | bytes 16777216 | tf_op jit(solution)/shard_map/all_to_all | solution.py:85
  211.6 198.0 %copy-start.1 = (f32[4,128,512]{2,1,0:T(8,128)S(1)}, f32[4,128,512]{2,1,0:T(8,128)}, u32[]{:S(2)}) copy-start(f32[4,128,512]{2,1,0:T(8,128)} %param.11) | copy-start | bytes 3145732
